TPU v7x, 32 devices: a whole 2x2x4 slice. The times are simulated.
32 devices in a mesh: groups: 2 (over y), chan: 8 (over z, x), sub: 2 (over core).
Axes of the slice: x: 2, y: 2, z: 4, core: 2. Of those that a mesh axis runs over, the one named last changes fastest.
Arguments:
- predicted_sky_response: bfloat16 [16384, 8, 2, 128], P(('groups', 'chan', 'sub')), parts along dimension 0, may hold values from -0.4375 to 0.4375
- measured_correlation: bfloat16 [16384, 2, 128], P(('groups', 'chan', 'sub')), parts along dimension 0, may hold values from -6 to 6
- keep_indicator: int32 [16384, 128], P(('groups', 'chan', 'sub')), parts along dimension 0, may hold values 0 or 1
- tile_owner: int32 [16384, 1], P(('groups', 'chan', 'sub')), parts along dimension 0, may hold values from 0 to 7; in each aligned block of 512 rows (0 to 511, 512 to 1023, ...) at most 192 rows name the same one
- tile_channel: int32 [16384], P(('groups', 'chan', 'sub')), parts along dimension 0, may hold values from 0 to 3
- tile_base: int32 [16384], P(('groups', 'chan', 'sub')), parts along dimension 0, may hold values from 0 to 14
- pairs: int32 [15, 2, 128], replicated, may hold values from 0 to 61, as said below
- gains: float32 [64, 2, 62, 8], P(('groups', 'chan')), parts along dimension 0, may hold values from -5 to 5
- duals: float32 [64, 2, 62, 8], P(('groups', 'chan', 'sub')), parts along dimension 0, may hold values from -4 to 4
- consensus: float32 [8, 2, 62, 8], P('groups'), parts along dimension 0, may hold values from -5 to 5
- rho: float32 [8], replicated, may hold values from 0.3 to 3
Outputs:
- gains_new: float32 [64, 2, 62, 8], P(('groups', 'chan', 'sub')), parts along dimension 0
- consensus_new: float32 [8, 2, 62, 8], P('groups'), parts along dimension 0
- duals_new: float32 [64, 2, 62, 8], P(('groups', 'chan', 'sub')), parts along dimension 0
There are 2 independent parts, one for each index of `groups`. A program takes and returns all parts, laid end to end along the dimension named above; an argument that names none is the same for every part. Nothing has to cross between parts.
Inputs may be any that keep to these rules, and one draw needn't show every extreme that they name: `tile_owner`: on the tiles of one device at most 192 name the same owner, a bound that some block reaches. `pairs`: the two stations of a row differ.
All inputs are finite; a program needn't handle non-finite values. No bound on the sum of `keep_indicator` on one device may be relied on, other than what follows from the above.
Results may differ from a plain program's by a relative error of at most 0.0027.
Values may be sent and summed in bfloat16 or wider, within the bound.
A program may use at most 128 MiB of HBM per device.

v0:
```python
import math
import jax
import jax.numpy as jnp
from jax import lax
from jax.sharding import PartitionSpec as P


def legendre_rows(channels):
    positions = jnp.arange(channels, dtype=jnp.float32)
    abscissa = (2.0 * positions - (channels - 1)) / max(channels - 1, 1)
    return jnp.stack(
        [
            jnp.ones_like(abscissa),
            abscissa,
            0.5 * (3.0 * abscissa * abscissa - 1.0),
            0.5 * (5.0 * abscissa * abscissa * abscissa - 3.0 * abscissa),
        ]
    )


def outer_terms(vector_real, vector_imag, weight_real, weight_imag):
    tiles_count, row_total_count, directions = vector_real.shape
    outer_real = (
        vector_real[..., :, None] * vector_real[..., None, :]
        + vector_imag[..., :, None] * vector_imag[..., None, :]
    )
    outer_imag = (
        vector_real[..., :, None] * vector_imag[..., None, :]
        - vector_imag[..., :, None] * vector_real[..., None, :]
    )
    normal = jnp.stack([outer_real, outer_imag], axis=2).reshape(
        tiles_count, row_total_count, 2 * directions * directions
    )
    side_real = vector_real * weight_real[..., None] + vector_imag * weight_imag[..., None]
    side_imag = vector_real * weight_imag[..., None] - vector_imag * weight_real[..., None]
    right_side = jnp.stack([side_real, side_imag], axis=2).reshape(
        tiles_count, row_total_count, 2 * directions
    )
    return (normal, right_side)


def row_terms(coupling, observed, near_gain, far_gain):
    coupling_real = jnp.swapaxes(coupling[:, :, 0, :], 1, 2).astype(jnp.float32)
    coupling_imag = jnp.swapaxes(coupling[:, :, 1, :], 1, 2).astype(jnp.float32)
    near_real, near_imag = (near_gain[:, :, 0, :], near_gain[:, :, 1, :])
    far_real, far_imag = (far_gain[:, :, 0, :], far_gain[:, :, 1, :])
    slope_real = coupling_real * far_real + coupling_imag * far_imag
    slope_imag = coupling_imag * far_real - coupling_real * far_imag
    mirror_real = coupling_real * near_real - coupling_imag * near_imag
    mirror_imag = -(coupling_real * near_imag + coupling_imag * near_real)
    model_real = jnp.sum(near_real * slope_real - near_imag * slope_imag, axis=-1)
    model_imag = jnp.sum(near_real * slope_imag + near_imag * slope_real, axis=-1)
    observed_f = observed.astype(jnp.float32)
    residual_real = observed_f[:, 0, :] - model_real
    residual_imag = observed_f[:, 1, :] - model_imag
    normal_near, right_near = outer_terms(slope_real, slope_imag, residual_real, residual_imag)
    normal_far, right_far = outer_terms(mirror_real, mirror_imag, residual_real, -residual_imag)
    normal = jnp.concatenate([normal_near, normal_far], axis=1).astype(jnp.bfloat16)
    right_side = jnp.concatenate([right_near, right_far], axis=1).astype(jnp.bfloat16)
    return (normal, right_side)


def tile_normals(coupling, observed, channel_index, base_index, pairs, gain_table):
    stations_count = gain_table.shape[2]
    stations = pairs[base_index]
    station_ids = jnp.arange(stations_count, dtype=jnp.int32)
    near_onehot = (stations[:, 0, :, None] == station_ids).astype(jnp.float32)
    far_onehot = (stations[:, 1, :, None] == station_ids).astype(jnp.float32)
    tile_gains = gain_table[channel_index]
    near_gain = jnp.einsum(
        "trs,tcsk->trck", near_onehot, tile_gains, precision=lax.Precision.HIGHEST
    )
    far_gain = jnp.einsum("trs,tcsk->trck", far_onehot, tile_gains, precision=lax.Precision.HIGHEST)
    normal, right_side = row_terms(coupling, observed, near_gain, far_gain)
    both_onehot = jnp.concatenate([near_onehot, far_onehot], axis=1).astype(jnp.bfloat16)
    tile_normal = jnp.einsum(
        "trs,trc->tsc", both_onehot, normal, preferred_element_type=jnp.float32
    )
    tile_right = jnp.einsum(
        "trs,trc->tsc", both_onehot, right_side, preferred_element_type=jnp.float32
    )
    return (tile_normal, tile_right)


def accumulate(coupling, observed, channel_index, base_index, pairs, gain_table, channel_slots):
    tiles_count = coupling.shape[0]
    block_size = math.gcd(tiles_count, 32)
    iteration_tally = tiles_count // block_size
    stations_count = gain_table.shape[2]
    directions = gain_table.shape[3]

    def one_step(totals, block_item):
        normal_acc, right_acc = totals
        tile_normal, tile_right = tile_normals(
            block_item[0], block_item[1], block_item[2], block_item[3], pairs, gain_table
        )
        return (
            (
                normal_acc.at[block_item[2]].add(tile_normal),
                right_acc.at[block_item[2]].add(tile_right),
            ),
            None,
        )

    block_items = (
        coupling.reshape((iteration_tally, block_size) + coupling.shape[1:]),
        observed.reshape((iteration_tally, block_size) + observed.shape[1:]),
        channel_index.reshape(iteration_tally, block_size),
        base_index.reshape(iteration_tally, block_size),
    )
    start_totals = (
        jnp.zeros((channel_slots, stations_count, 2 * directions * directions), jnp.float32),
        jnp.zeros((channel_slots, stations_count, 2 * directions), jnp.float32),
    )
    (normal_sum, right_sum), _ = lax.scan(one_step, start_totals, block_items)
    return (normal_sum, right_sum)


def admm_update(normal, right_side, gain, dual, anchor, rho):
    count, stations = (normal.shape[0], normal.shape[1])
    directions = rho.shape[0]
    normal_blocks = normal.reshape(count, stations, 2, directions, directions)
    ridge_diag = jnp.diag(rho)
    higher_half_records = jnp.concatenate(
        [normal_blocks[:, :, 0] + ridge_diag, -normal_blocks[:, :, 1]], axis=-1
    )
    lower_rows = jnp.concatenate(
        [normal_blocks[:, :, 1], normal_blocks[:, :, 0] + ridge_diag], axis=-1
    )
    system = jnp.concatenate([higher_half_records, lower_rows], axis=-2)
    gain_rows = jnp.transpose(gain, (0, 2, 1, 3))
    dual_rows = jnp.transpose(dual, (0, 2, 1, 3))
    anchor_rows = jnp.transpose(anchor, (0, 2, 1, 3))
    target = (
        right_side.reshape(count, stations, 2, directions)
        - dual_rows
        - rho * (gain_rows - anchor_rows)
    )
    factor = jnp.linalg.cholesky(system)
    gain_step = jax.scipy.linalg.cho_solve(
        (factor, True), target.reshape(count, stations, 2 * directions)[..., None]
    )[..., 0]
    return gain + jnp.transpose(gain_step.reshape(count, stations, 2, directions), (0, 2, 1, 3))


def fit_consensus(poly_basis, summed):
    gram_matrix = jnp.dot(poly_basis, poly_basis.T, precision=lax.Precision.HIGHEST)
    factor = jnp.linalg.cholesky(gram_matrix)
    coeffs = jax.scipy.linalg.cho_solve((factor, True), summed.reshape(summed.shape[0], -1))
    return coeffs.reshape(summed.shape)


def body(
    predicted_sky_response,
    measured_correlation,
    keep_indicator,
    tile_owner,
    tile_channel,
    tile_base,
    pairs,
    gains,
    duals,
    consensus,
    rho,
):
    channels_here = gains.shape[0]
    chan_count = lax.axis_size("chan")
    sub_count = lax.axis_size("sub")
    half_count = channels_here // sub_count
    retained_selector = keep_indicator > 0
    predicted_response_kept = jnp.where(
        retained_selector[:, None, None, :],
        predicted_sky_response,
        jnp.zeros_like(predicted_sky_response),
    )
    measured_correlation_kept = jnp.where(
        retained_selector[:, None, :], measured_correlation, jnp.zeros_like(measured_correlation)
    )
    owner_index = tile_owner[:, 0]
    all_gains = lax.all_gather(gains, "chan", axis=0, tiled=True)
    full_channel = owner_index * channels_here + tile_channel
    normal_sum, right_sum = accumulate(
        predicted_response_kept,
        measured_correlation_kept,
        full_channel,
        tile_base,
        pairs,
        all_gains,
        channels_here * chan_count,
    )
    normal_part, right_part = (
        lax.psum_scatter(normal_sum, ("chan", "sub"), scatter_dimension=0, tiled=True),
        lax.psum_scatter(right_sum, ("chan", "sub"), scatter_dimension=0, tiled=True),
    )
    sub_index = lax.axis_index("sub")
    chan_index = lax.axis_index("chan")
    my_gains = lax.dynamic_slice_in_dim(gains, sub_index * half_count, half_count, 0)
    poly_basis = legendre_rows(channels_here * chan_count)
    first_channel = (chan_index * sub_count + sub_index) * half_count
    my_basis = lax.dynamic_slice_in_dim(poly_basis, first_channel, half_count, 1)
    anchor = jnp.einsum("df,dcsk->fcsk", my_basis, consensus, precision=lax.Precision.HIGHEST)
    gains_new = admm_update(normal_part, right_part, my_gains, duals, anchor, rho)
    partial_value = jnp.einsum(
        "df,fcsk->dcsk", my_basis, gains_new + duals / rho, precision=lax.Precision.HIGHEST
    )
    summed = lax.psum(partial_value, ("chan", "sub"))
    consensus_new = fit_consensus(poly_basis, summed)
    duals_new = duals + rho * (
        gains_new
        - jnp.einsum("df,dcsk->fcsk", my_basis, consensus_new, precision=lax.Precision.HIGHEST)
    )
    return (gains_new, consensus_new, duals_new)


def solution(mesh):
    placed = (
        P(("groups", "chan", "sub"), None, None, None),
        P(("groups", "chan", "sub"), None, None),
        P(("groups", "chan", "sub"), None),
        P(("groups", "chan", "sub"), None),
        P(("groups", "chan", "sub")),
        P(("groups", "chan", "sub")),
        P(),
        P(("groups", "chan"), None, None, None),
        P(("groups", "chan", "sub"), None, None, None),
        P("groups", None, None, None),
        P(),
    )
    return jax.shard_map(
        body,
        mesh=mesh,
        in_specs=placed,
        out_specs=(
            P(("groups", "chan", "sub"), None, None, None),
            P("groups", None, None, None),
            P(("groups", "chan", "sub"), None, None, None),
        ),
        check_vma=False,
    )
```

profile of v0, /device:TPU:0, one launch (start us, length us, event | category | flops | bytes accessed | tf_op | source)
XLA Modules:
  0.0 650.6 jit_solution(18375419178991925934)
XLA Ops:
  8.3 3.6 copy_select_fusion
  12.0 32.6 %all_gather.3 = f32[32,2,62,8]{2,3,1,0:T(8,128)S(1)} all-gather(f32[4,2,62,8]{2,3,1,0:T(8,128)S(1)} %copy-done.8), channel_id=1, replica_groups=mesh['groups'=2,'chan'=8,'sub'=2] {'chan'}, dimensions={0}, use_global_device_ids=true | all-gather | bytes 142848 | tf_op jit(solution)/shard_map/all_gather | solution.py:180
  44.9 225.0 %while.12 = (s32[]{:T(128)}, f32[32,62,128]{2,1,0:T(8,128)S(1)}, f32[32,62,16]{1,2,0:T(8,128)S(1)}, s32[16,32]{1,0:T(8,128)S(1)}, s32[16,32]{1,0:T(8,128)S(1)}, ...) while((s32[]{:T(128)}, f32[32,62,128]{2,1,0:T(8,128)S(1)}, ...), condition=%wide.region_5.6_spmd, body=%wide.region_0.5_spmd.sunk | while | flops 259593408 | bytes 28256220 | solution.py:115
  49.5 1.8 scatter_fusion.1
  54.8 2.0 fusion.100
  56.8 2.1 scatter_fusion
  63.5 1.8 scatter_fusion.1
  68.8 2.0 fusion.100
  70.8 2.1 scatter_fusion
  82.9 2.0 fusion.100
  84.9 2.1 scatter_fusion
  96.9 2.0 fusion.100
  98.9 2.1 scatter_fusion
  111.0 2.0 fusion.100
  113.0 2.1 scatter_fusion
  119.8 1.8 scatter_fusion.1
  125.1 2.0 fusion.100
  127.1 2.1 scatter_fusion
  139.1 2.0 fusion.100
  141.1 2.1 scatter_fusion
  153.2 2.0 fusion.100
  155.2 2.1 scatter_fusion
  167.2 2.0 fusion.100
  169.2 2.1 scatter_fusion
  176.0 1.8 scatter_fusion.1
  181.3 2.0 fusion.100
  183.3 2.1 scatter_fusion
  190.1 1.8 scatter_fusion.1
  195.4 2.0 fusion.100
  197.4 2.1 scatter_fusion
  209.4 2.0 fusion.100
  211.4 2.1 scatter_fusion
  223.5 2.0 fusion.100
  225.5 2.1 scatter_fusion
  232.2 1.8 scatter_fusion.1
  237.5 2.0 fusion.100
  239.5 2.1 scatter_fusion
  246.3 1.8 scatter_fusion.1
  251.6 2.0 fusion.100
  253.6 2.1 scatter_fusion
  265.7 2.0 fusion.100
  267.7 2.1 scatter_fusion
  270.6 2.0 copy.113
  275.2 52.2 %reduce-scatter.5.cloned.1.call-done = f32[2,62,16]{1,2,0:T(8,128)} async-done(((f32[32,62,16]{1,2,0:T(8,128)}), f32[2,62,16]{1,2,0:T(8,128)}) %reduce-scatter.5.cloned.1.call-update) | async-done | bytes 7952 | tf_op jit(solution)/shard_map/reduce_scatter | solution.py:193
  328.5 63.5 %reduce-scatter.3.cloned.1.call-done = f32[2,62,128]{1,2,0:T(8,128)} async-done(((f32[32,62,128]{1,2,0:T(8,128)}), f32[2,62,128]{1,2,0:T(8,128)}) %reduce-scatter.3.cloned.1.call-update) | async-done | bytes 63504 | tf_op jit(solution)/shard_map/reduce_scatter | solution.py:192
  394.5 181.8 %custom-call.21 = f32[2,62,16,16]{3,2,1,0:T(8,128)S(1)} custom-call(f32[2,62,16,16]{3,2,1,0:T(8,128)S(1)} %broadcast_multiply_fusion), custom_call_target="Cholesky" | custom-call | tf_op jit(solution)/shard_map/jit(cholesky)/cholesky | solution.py:139
  577.0 5.4 custom-call.22
  583.5 57.6 %psum.7 = f32[2,62,8,4]{1,3,2,0:T(4,128)S(1)} all-reduce(f32[2,62,8,4]{1,3,2,0:T(4,128)S(1)} %copy.126), channel_id=1, replica_groups=mesh['groups'=2,'chan'=8,'sub'=2] {'chan','sub'}, use_global_device_ids=true, to_apply=%region_12.13 | all-reduce | flops 3968 | bytes 31744 | tf_op jit(solution)/shard_map/psum | solution.py:206
  (613 shorter events, 155.8 us)
Async XLA Ops:
  7.2 320.9 %copy-start = (f32[4,2,62,8]{2,3,1,0:T(8,128)S(1)}, f32[4,2,62,8]{2,3,1,0:T(8,128)}, u32[]{:S(2)}) copy-start(f32[4,2,62,8]{2,3,1,0:T(8,128)} %param.22) | copy-start | bytes 47620
  7.2 320.2 %reduce-scatter.5.cloned.1.call-start = ((), (), s32[]{:S(2)}) async-start(), calls=%async_computation.3 | async-start | bytes 278528 | tf_op jit(solution)/shard_map/reduce_scatter | solution.py:193
  8.2 3.7 copy-start.7
  8.2 3.7 copy-start.8
  8.2 36.3 %copy-start.11 = (s32[512,1]{0,1:T(1,128)S(1)}, s32[512,1]{0,1:T(1,128)}, u32[]{:S(2)}) copy-start(s32[512,1]{0,1:T(1,128)} %param.16) | copy-start | bytes 6148
  8.3 36.3 %copy-start.9 = (s32[512]{0:T(512)S(1)}, s32[512]{0:T(512)}, u32[]{:S(2)}) copy-start(s32[512]{0:T(512)} %param.17) | copy-start | bytes 6148
  8.3 36.4 %copy-start.10 = (s32[512]{0:T(512)S(1)}, s32[512]{0:T(512)}, u32[]{:S(2)}) copy-start(s32[512]{0:T(512)} %param.18) | copy-start | bytes 6148
  11.9 33.0 %copy-start.4 = (s32[15,2,128]{2,1,0:T(2,128)S(1)}, s32[15,2,128]{2,1,0:T(2,128)}, u32[]{:S(2)}) copy-start(s32[15,2,128]{2,1,0:T(2,128)} %param.19) | copy-start | bytes 46084
  44.9 3.7 copy-start.5
  49.1 2.1 copy-start.2
  56.8 2.2 copy-start.6
  58.9 3.7 copy-start.5
  63.2 2.1 copy-start.2
  70.8 2.2 copy-start.6
  73.0 3.7 copy-start.5
  84.9 2.1 copy-start.6
  87.0 3.7 copy-start.5
  98.9 2.1 copy-start.6
  101.1 3.7 copy-start.5
  113.0 2.2 copy-start.6
  115.2 3.7 copy-start.5
  127.0 2.2 copy-start.6
  129.2 3.7 copy-start.5
  141.1 2.2 copy-start.6
  143.3 3.7 copy-start.5
  155.2 2.2 copy-start.6
  157.3 3.7 copy-start.5
  169.2 2.2 copy-start.6
  171.4 3.7 copy-start.5
  175.6 2.1 copy-start.2
  183.3 2.2 copy-start.6
  185.5 3.7 copy-start.5
  189.7 2.1 copy-start.2
  197.3 2.2 copy-start.6
  199.5 3.7 copy-start.5
  211.4 2.2 copy-start.6
  213.6 3.7 copy-start.5
  225.5 2.1 copy-start.6
  227.6 3.7 copy-start.5
  231.9 2.1 copy-start.2
  239.5 2.2 copy-start.6
  241.7 3.7 copy-start.5
  253.6 2.2 copy-start.6
  255.8 3.7 copy-start.5
  267.7 2.2 copy-start.6
  270.6 121.4 %reduce-scatter.3.cloned.1.call-start = ((), (), s32[]{:S(2)}) async-start(), calls=%async_computation.2 | async-start | bytes 2228224 | tf_op jit(solution)/shard_map/reduce_scatter | solution.py:192
  270.6 4.5 copy-start.12
  270.6 57.5 %copy-start.13 = (f32[2,2,62,8]{2,3,1,0:T(8,128)S(1)}, f32[2,2,62,8]{2,3,1,0:T(8,128)}, u32[]{:S(2)}) copy-start(f32[2,2,62,8]{2,3,1,0:T(8,128)} %param.21) | copy-start | bytes 23812
  (28 other events, 47.4 us)
Sparse Core Ops, SparseCore 0:
  270.7 56.6 reduce-scatter.4
  331.1 60.8 reduce-scatter.2
where the time goes:
time: 652 us; the launch traced here: 651 us
  other arithmetic  281 us (43%)
  waiting for transfers between devices  116 us (18%)
  blocking collectives  90.2 us (14%)
  local copies, waits for them, and re-layouts  85.5 us (13%)
  matrix products  59.6 us (9%)
  between operations  14.4 us (2%)
    another operation x4, other arithmetic, admm_update(): factor = jnp.linalg.cholesky(system)  182 us
    reduce_scatter x1, waiting for transfers between devices, body(): lax.psum_scatter(normal_sum, ('chan', 'sub'), scatter_dimension=0, tiled=...  63.5 us
    psum x1, blocking collectives, body(): summed = lax.psum(partial_value, ('chan', 'sub'))  57.6 us
    reduce_scatter x1, waiting for transfers between devices, body(): lax.psum_scatter(right_sum, ('chan', 'sub'), scatter_dimension=0, tiled=T...  52.2 us
    reshape x32, local copies, waits for them, and re-layouts, outer_terms(): jnp.stack([outer_real, outer_imag], axis=2)  42.6 us
    scatter-add x16, other arithmetic, one_step(): normal_acc.at[block_item[2]].add(tile_normal)  34.1 us
    all_gather x1, blocking collectives, body(): all_gains = lax.all_gather(gains, 'chan', axis=0, tiled=True)  32.6 us
    dot_general x16, matrix products, tile_normals(): jnp.einsum('trs,trc->tsc', both_onehot, normal, preferred_element_type=jn...  31.6 us
  transfers between devices with their start and end apart: 2, of which 2 were waited for; matrix products, arithmetic and copies ran while one was open for 1% of the time, Pallas kernels for 0%

commit v1 on v0

--- a/solution.py
+++ b/solution.py
@@ -203,7 +203,7 @@
     partial_value = jnp.einsum(
         "df,fcsk->dcsk", my_basis, gains_new + duals / rho, precision=lax.Precision.HIGHEST
     )
-    summed = lax.psum(partial_value, ("chan", "sub"))
+    summed = jnp.sum(lax.all_gather(partial_value, ("chan", "sub")), axis=0)
     consensus_new = fit_consensus(poly_basis, summed)
     duals_new = duals + rho * (
         gains_new

time: 652 us -> 615 us (0.943)
  blocking collectives: 90.2 us -> 53.3 us
    psum x1 -> x0, blocking collectives: 57.6 us -> none  [body(): summed = lax.psum(partial_value, ('chan', 'sub'))]
    all_gather x0 -> x1, blocking collectives: none -> 20.7 us  [body(): summed = jnp.sum(lax.all_gather(partial_value, ('chan', 'sub')), axis=0)]
where the time goes in v1:
time: 615 us; the launch traced here: 614 us
  other arithmetic  281 us (46%)
  waiting for transfers between devices  116 us (19%)
  local copies, waits for them, and re-layouts  85.5 us (14%)
  matrix products  59.7 us (10%)
  blocking collectives  53.3 us (9%)
  between operations  14.4 us (2%)
    another operation x4, other arithmetic, admm_update(): factor = jnp.linalg.cholesky(system)  182 us
    reduce_scatter x1, waiting for transfers between devices, body(): lax.psum_scatter(normal_sum, ('chan', 'sub'), scatter_dimension=0, tiled=...  63.5 us
    reduce_scatter x1, waiting for transfers between devices, body(): lax.psum_scatter(right_sum, ('chan', 'sub'), scatter_dimension=0, tiled=T...  52.2 us
    reshape x32, local copies, waits for them, and re-layouts, outer_terms(): jnp.stack([outer_real, outer_imag], axis=2)  42.6 us
    scatter-add x16, other arithmetic, one_step(): normal_acc.at[block_item[2]].add(tile_normal)  34.1 us
    all_gather x1, blocking collectives, body(): all_gains = lax.all_gather(gains, 'chan', axis=0, tiled=True)  32.6 us
    dot_general x16, matrix products, tile_normals(): jnp.einsum('trs,trc->tsc', both_onehot, normal, preferred_element_type=jn...  31.6 us
    scatter-add x16, other arithmetic, one_step(): right_acc.at[block_item[2]].add(tile_right)  27.9 us
  transfers between devices with their start and end apart: 2, of which 2 were waited for; matrix products, arithmetic and copies ran while one was open for 1% of the time, Pallas kernels for 0%

profile of v1, /device:TPU:0, one launch (start us, length us, event | category | flops | bytes accessed | tf_op | source)
XLA Modules:
  0.0 613.8 jit_solution(2138049456885429738)
XLA Ops:
  8.3 3.6 copy_select_fusion
  12.0 32.6 %all_gather.9 = f32[32,2,62,8]{2,3,1,0:T(8,128)S(1)} all-gather(f32[4,2,62,8]{2,3,1,0:T(8,128)S(1)} %copy-done.8), channel_id=1, replica_groups=mesh['groups'=2,'chan'=8,'sub'=2] {'chan'}, dimensions={0}, use_global_device_ids=true | all-gather | bytes 142848 | tf_op jit(solution)/shard_map/all_gather | solution.py:180
  44.9 225.0 %while.12 = (s32[]{:T(128)}, f32[32,62,128]{2,1,0:T(8,128)S(1)}, f32[32,62,16]{1,2,0:T(8,128)S(1)}, s32[16,32]{1,0:T(8,128)S(1)}, s32[16,32]{1,0:T(8,128)S(1)}, ...) while((s32[]{:T(128)}, f32[32,62,128]{2,1,0:T(8,128)S(1)}, ...), condition=%wide.region_5.6_spmd, body=%wide.region_0.5_spmd.sunk | while | flops 259593408 | bytes 28256220 | solution.py:115
  49.5 1.8 scatter_fusion.1
  54.8 2.0 fusion.100
  56.8 2.1 scatter_fusion
  63.5 1.8 scatter_fusion.1
  68.8 2.0 fusion.100
  70.8 2.1 scatter_fusion
  82.9 2.0 fusion.100
  84.9 2.1 scatter_fusion
  96.9 2.0 fusion.100
  98.9 2.1 scatter_fusion
  111.0 2.0 fusion.100
  113.0 2.1 scatter_fusion
  119.8 1.8 scatter_fusion.1
  125.1 2.0 fusion.100
  127.1 2.1 scatter_fusion
  139.1 2.0 fusion.100
  141.1 2.1 scatter_fusion
  153.2 2.0 fusion.100
  155.2 2.1 scatter_fusion
  167.2 2.0 fusion.100
  169.2 2.1 scatter_fusion
  176.0 1.8 scatter_fusion.1
  181.3 2.0 fusion.100
  183.3 2.1 scatter_fusion
  190.1 1.8 scatter_fusion.1
  195.4 2.0 fusion.100
  197.4 2.1 scatter_fusion
  209.4 2.0 fusion.100
  211.4 2.1 scatter_fusion
  223.5 2.0 fusion.100
  225.5 2.1 scatter_fusion
  232.2 1.8 scatter_fusion.1
  237.5 2.0 fusion.100
  239.5 2.1 scatter_fusion
  246.3 1.8 scatter_fusion.1
  251.6 2.0 fusion.100
  253.6 2.1 scatter_fusion
  265.7 2.0 fusion.100
  267.7 2.1 scatter_fusion
  270.6 2.0 copy.114
  275.2 52.2 %reduce-scatter.5.cloned.1.call-done = f32[2,62,16]{1,2,0:T(8,128)} async-done(((f32[32,62,16]{1,2,0:T(8,128)}), f32[2,62,16]{1,2,0:T(8,128)}) %reduce-scatter.5.cloned.1.call-update) | async-done | bytes 7952 | tf_op jit(solution)/shard_map/reduce_scatter | solution.py:193
  328.5 63.5 %reduce-scatter.3.cloned.1.call-done = f32[2,62,128]{1,2,0:T(8,128)} async-done(((f32[32,62,128]{1,2,0:T(8,128)}), f32[2,62,128]{1,2,0:T(8,128)}) %reduce-scatter.3.cloned.1.call-update) | async-done | bytes 63504 | tf_op jit(solution)/shard_map/reduce_scatter | solution.py:192
  394.5 181.8 %custom-call.21 = f32[2,62,16,16]{3,2,1,0:T(8,128)S(1)} custom-call(f32[2,62,16,16]{3,2,1,0:T(8,128)S(1)} %broadcast_multiply_fusion), custom_call_target="Cholesky" | custom-call | tf_op jit(solution)/shard_map/jit(cholesky)/cholesky | solution.py:139
  577.0 5.4 custom-call.22
  582.9 20.7 %all-gather = f32[64,2,62,8]{2,3,1,0:T(8,128)S(1)} all-gather(f32[4,2,62,8]{2,3,1,0:T(8,128)S(1)} %copy.126), channel_id=2, replica_groups=mesh['groups'=2,'chan'=8,'sub'=2] {'chan','sub'}, dimensions={0}, use_global_device_ids=true | all-gather | bytes 269824 | tf_op jit(solution)/shard_map/all_gather | solution.py:206
  (615 shorter events, 155.8 us)
Async XLA Ops:
  7.2 320.9 %copy-start = (f32[4,2,62,8]{2,3,1,0:T(8,128)S(1)}, f32[4,2,62,8]{2,3,1,0:T(8,128)}, u32[]{:S(2)}) copy-start(f32[4,2,62,8]{2,3,1,0:T(8,128)} %param.22) | copy-start | bytes 47620
  7.2 320.2 %reduce-scatter.5.cloned.1.call-start = ((), (), s32[]{:S(2)}) async-start(), calls=%async_computation.3 | async-start | bytes 278528 | tf_op jit(solution)/shard_map/reduce_scatter | solution.py:193
  8.2 3.7 copy-start.7
  8.2 3.7 copy-start.8
  8.2 36.3 %copy-start.11 = (s32[512,1]{0,1:T(1,128)S(1)}, s32[512,1]{0,1:T(1,128)}, u32[]{:S(2)}) copy-start(s32[512,1]{0,1:T(1,128)} %param.16) | copy-start | bytes 6148
  8.3 36.3 %copy-start.9 = (s32[512]{0:T(512)S(1)}, s32[512]{0:T(512)}, u32[]{:S(2)}) copy-start(s32[512]{0:T(512)} %param.17) | copy-start | bytes 6148
  8.3 36.4 %copy-start.10 = (s32[512]{0:T(512)S(1)}, s32[512]{0:T(512)}, u32[]{:S(2)}) copy-start(s32[512]{0:T(512)} %param.18) | copy-start | bytes 6148
  11.9 33.0 %copy-start.4 = (s32[15,2,128]{2,1,0:T(2,128)S(1)}, s32[15,2,128]{2,1,0:T(2,128)}, u32[]{:S(2)}) copy-start(s32[15,2,128]{2,1,0:T(2,128)} %param.19) | copy-start | bytes 46084
  44.9 3.7 copy-start.5
  49.1 2.1 copy-start.2
  56.8 2.2 copy-start.6
  58.9 3.7 copy-start.5
  63.2 2.1 copy-start.2
  70.8 2.2 copy-start.6
  73.0 3.7 copy-start.5
  84.9 2.1 copy-start.6
  87.0 3.7 copy-start.5
  98.9 2.1 copy-start.6
  101.1 3.7 copy-start.5
  113.0 2.2 copy-start.6
  115.2 3.7 copy-start.5
  127.0 2.2 copy-start.6
  129.2 3.7 copy-start.5
  141.1 2.2 copy-start.6
  143.3 3.7 copy-start.5
  155.2 2.2 copy-start.6
  157.3 3.7 copy-start.5
  169.2 2.2 copy-start.6
  171.4 3.7 copy-start.5
  175.6 2.1 copy-start.2
  183.3 2.2 copy-start.6
  185.5 3.7 copy-start.5
  189.7 2.1 copy-start.2
  197.3 2.2 copy-start.6
  199.5 3.7 copy-start.5
  211.4 2.2 copy-start.6
  213.6 3.7 copy-start.5
  225.5 2.1 copy-start.6
  227.6 3.7 copy-start.5
  231.9 2.1 copy-start.2
  239.5 2.2 copy-start.6
  241.7 3.7 copy-start.5
  253.6 2.2 copy-start.6
  255.8 3.7 copy-start.5
  267.7 2.2 copy-start.6
  270.6 121.4 %reduce-scatter.3.cloned.1.call-start = ((), (), s32[]{:S(2)}) async-start(), calls=%async_computation.2 | async-start | bytes 2228224 | tf_op jit(solution)/shard_map/reduce_scatter | solution.py:192
  270.6 4.5 copy-start.12
  270.6 57.5 %copy-start.13 = (f32[2,2,62,8]{2,3,1,0:T(8,128)S(1)}, f32[2,2,62,8]{2,3,1,0:T(8,128)}, u32[]{:S(2)}) copy-start(f32[2,2,62,8]{2,3,1,0:T(8,128)} %param.21) | copy-start | bytes 23812
  (28 other events, 47.4 us)
Sparse Core Ops, SparseCore 0:
  270.7 56.6 reduce-scatter.4
  331.1 60.8 reduce-scatter.2
